TPU v7x, 32 devices: a whole 2x2x4 slice. The times are simulated.
32 devices in a mesh: groups: 2 (over y), gx: 4 (over z), gy: 4 (over x, core).
Axes of the slice: x: 2, y: 2, z: 4, core: 2. Of those that a mesh axis runs over, the one named last changes fastest.
Arguments:
- tokens: bfloat16 [2, 16, 16384], P(None, 'groups', 'gx'), parts along dimension 1, may hold values from -20 to 20, as said below
- lengths: int32 [2, 16], P(None, ('groups', 'gx')), parts along dimension 1, may hold values from 1 to 1024, as said below
- norm_gain: bfloat16 [16384], P('gx'), may hold values from 0.5 to 2
- w_query: bfloat16 [16384, 8192], P('gx', 'gy'), may hold values from -1.171875 to 1.171875
- key_value_weight: bfloat16 [16384, 4, 256], P('gx', 'gy'), may hold values from -0.046875 to 0.046875
- w_out: bfloat16 [8192, 16384], P('gy', 'gx'), may hold values from -0.0625 to 0.0625
- cache: bfloat16 [2, 16, 1024, 4, 2, 128], P(None, ('groups', 'gx'), None, 'gy'), parts along dimension 1, may hold values from -16 to 16
Outputs:
- layer_out: bfloat16 [2, 16, 16384], P(None, 'groups', 'gx'), parts along dimension 1
There are 2 independent parts, one for each index of `groups`. A program takes and returns all parts, laid end to end along the dimension named above; an argument that names none is the same for every part. Nothing has to cross between parts.
Inputs may be any that keep to these rules, and one draw needn't show every extreme that they name: `tokens`: entries vary with the feature and the row. `lengths`: some rollout has exactly 1024 cached positions in every draw.
All inputs are finite; a program needn't handle non-finite values.
Results may differ from a plain program's by a relative error of at most 0.012.
The roundings to bfloat16 on the way count: a program that leaves them out, or rounds other values in their place, can miss the bound.
Values may be sent and summed in bfloat16 or wider, within the bound.
No kernel may reach another device: no remote copies, remote signals or barrier semaphores. Data moves between devices by JAX's collectives and lax.ppermute only.
A program may use at most 128 MiB of HBM per device.

v0:
```python
import jax
import jax.numpy as jnp
from jax import lax
from jax.sharding import PartitionSpec as P

MODEL_WIDTH = 16384
HEAD_SIZE = 128


def rotate(vectors, positions):
    half = vectors.shape[-1] // 2
    freq = 500000.0 ** (-2.0 * jnp.arange(half, dtype=jnp.float32) / vectors.shape[-1])
    angle = positions[..., None] * freq
    cosine = jnp.cos(angle)
    sine = jnp.sin(angle)
    first = vectors[..., :half]
    second = vectors[..., half:]
    return jnp.concatenate(
        [first * cosine - second * sine, second * cosine + first * sine], axis=-1
    )


def attend(query_sum, keyval_sum, local_squares, lengths, cache):
    batches, rows_here = lengths.shape
    score_scale = lax.rsqrt(local_squares / MODEL_WIDTH + 1e-05)
    heads_kv = keyval_sum.shape[2]
    query_group = query_sum.shape[2] // (heads_kv * HEAD_SIZE)
    query = (
        query_sum.reshape(batches, rows_here, heads_kv, query_group, HEAD_SIZE)
        * score_scale[:, :, None, None, None]
    )
    key_value = keyval_sum * score_scale[:, :, None, None]
    positions = lengths.astype(jnp.float32)
    rotated_query = rotate(query, positions[:, :, None, None]).astype(jnp.bfloat16)
    rkey = rotate(key_value[..., :HEAD_SIZE], positions[:, :, None])
    value_new = key_value[..., HEAD_SIZE:]
    inv_root = 1.0 / jnp.sqrt(jnp.float32(HEAD_SIZE))
    keys = cache[:, :, :, :, 0, :]
    values = cache[:, :, :, :, 1, :]
    scores = (
        jnp.einsum("mrkgd,mrskd->mrkgs", rotated_query, keys, preferred_element_type=jnp.float32)
        * inv_root
    )
    valid = jnp.arange(cache.shape[2], dtype=jnp.int32)[None, None, :] < lengths[:, :, None]
    scores = jnp.where(valid[:, :, None, None, :], scores, -1e30)
    new_score = (
        jnp.sum(rotated_query.astype(jnp.float32) * rkey[:, :, :, None, :], axis=-1) * inv_root
    )
    top = jnp.maximum(jnp.max(scores, axis=-1), new_score)
    weights = jnp.exp(scores - top[..., None])
    new_weight = jnp.exp(new_score - top)
    total = jnp.sum(weights, axis=-1) + new_weight
    summed = jnp.einsum(
        "mrkgs,mrskd->mrkgd",
        weights.astype(jnp.bfloat16),
        values,
        preferred_element_type=jnp.float32,
    )
    summed = summed + new_weight[..., None] * value_new[:, :, :, None, :]
    return (
        (summed / total[..., None])
        .astype(jnp.bfloat16)
        .reshape(batches, rows_here, heads_kv * query_group * HEAD_SIZE)
    )


def local(tokens, lengths, norm_gain, w_query, key_value_weight, w_out, cache):
    x_full = tokens.astype(jnp.float32)
    squares = jnp.sum(x_full * x_full, axis=-1)
    normed = (x_full * norm_gain.astype(jnp.float32)).astype(jnp.bfloat16)
    query_part = jnp.einsum("mrd,dc->mrc", normed, w_query, preferred_element_type=jnp.float32)
    keyval_part = jnp.einsum(
        "mrd,dkc->mrkc", normed, key_value_weight, preferred_element_type=jnp.float32
    )
    query_sum, keyval_sum, local_squares = (
        lax.psum_scatter(query_part, "gx", scatter_dimension=1, tiled=True),
        lax.psum_scatter(keyval_part, "gx", scatter_dimension=1, tiled=True),
        lax.psum_scatter(squares, "gx", scatter_dimension=1, tiled=True),
    )
    attended = attend(query_sum, keyval_sum, local_squares, lengths, cache)
    projected = jnp.einsum(
        "mrc,cd->mrd",
        lax.all_gather(attended, "gx", axis=1, tiled=True),
        w_out,
        preferred_element_type=jnp.float32,
    )
    summed_heads = lax.psum(projected, "gy")
    return (x_full + summed_heads).astype(jnp.bfloat16)


def solution(mesh):
    placed = (
        P(None, "groups", "gx"),
        P(None, ("groups", "gx")),
        P("gx"),
        P("gx", "gy"),
        P("gx", "gy", None),
        P("gy", "gx"),
        P(None, ("groups", "gx"), None, "gy", None, None),
    )
    return jax.shard_map(
        local, mesh=mesh, in_specs=placed, out_specs=P(None, "groups", "gx"), check_vma=False
    )
```

profile of v0, /device:TPU:0, one launch (start us, length us, event | category | flops | bytes accessed | tf_op | source)
XLA Modules:
  0.0 122.0 jit_solution(11372717634072038642)
XLA Ops:
  6.5 0.8 convert_element_type.46
  7.4 8.8 %fusion.2 = f32[2,8,2048]{2,1,0:T(8,128)} fusion(bf16[4096,2048]{1,0:T(8,128)(2,1)} %param.10, bf16[2,8,4096]{2,1,0:T(8,128)(2,1)} %param.7, f32[4096]{0:T(1024)S(1)} %convert_element_type.46), kind=kOutput, calls=%fused_computation.2 | convolution fusion | flops 268632064 | bytes 17055744 | tf_op jit(solution)/shard_map/mrd,dc->mrc/dot_general | solution.py:71
  16.3 0.1 fusion.13
  16.4 0.1 iota_compare_fusion
  16.5 0.4 fusion.9
  16.9 0.7 dynamic-slice
  18.3 0.1 multiply_cosine_fusion.1
  18.4 20.8 %all-reduce.3 = (f32[2,8]{1,0:T(2,128)S(1)}, f32[2,8,1,256]{3,1,0,2:T(8,128)S(1)}) all-reduce(f32[2,8]{1,0:T(2,128)S(1)} %fusion.13, f32[2,8,1,256]{3,1,0,2:T(8,128)S(1)} %fusion.9), channel_id=3, replica_groups=mesh['groups'=2,'gx'=4,'gy'=4] {'gx'}, use_global_device_ids=true, to_apply=%region_2.0.clone | all-reduce | flops 4112 | bytes 32896
  39.2 0.1 fusion.32
  39.3 0.1 dynamic-slice_multiply_fusion
  39.4 0.1 fusion.29
  39.5 6.9 %fusion.35 = (bf16[2,2,1024,1,1,128]{5,4,3,2,1,0:T(2,128)(2,1)}, bf16[2,2,1024,1,1,128]{5,4,3,2,1,0:T(2,128)(2,1)}) fusion(bf16[2,2,1024,1,2,128]{5,4,3,2,1,0:T(2,128)(2,1)} %param.13), kind=kLoop, calls=%fused_computation.55 | loop fusion | bytes 4194304 | tf_op jit(solution)/shard_map/slice | solution.py:38
  46.4 0.1 maximum_bitcast_fusion
  46.5 7.3 %all-reduce.9.cloned.1.call-done = f32[2,8,2048]{2,1,0:T(8,128)} async-done(((f32[2,8,2048]{2,1,0:T(8,128)}), f32[2,8,2048]{2,1,0:T(8,128)}) %all-reduce.9.cloned.1.call-update) | async-done | bytes 131088
  53.9 0.9 constant_dynamic-slice_fusion
  54.9 0.1 subtract_convert_fusion
  55.0 0.2 multiply_reduce_fusion
  55.1 2.1 %fusion.36 = (f32[2,2,16]{2,1,0:T(2,128)S(1)}, f32[2,2,16,1024]{3,2,1,0:T(8,128)S(1)}) fusion(bf16[2,2,1024,1,1,128]{5,4,3,2,1,0:T(2,128)(2,1)} %get-tuple-element.9, bf16[2,2,16,64]{3,2,1,0:T(8,128)(2,1)S(1)} %bitcast.38, bf16[2,2,16,64]{3,2,1,0:T(8,128)(2,1)S(1)} %bitcast.37, pred[2,2,1024]{2,1,0:T(4,128)(4,1)S(1)} %iota_compare_fusion), kind=kOutput, calls=%fused_computation.56 | convolution fusion | flops 17006528 | bytes 1331456 | tf_op jit(solution)/shard_map/mrkgd,mrskd->mrkgs/dot_general | solution.py:41
  57.3 0.2 fusion.15
  57.5 1.9 %fusion.8 = bf16[2,2,16,128]{3,2,1,0:T(8,128)(2,1)S(1)} fusion(bf16[2,2,1024,1,1,128]{5,4,3,2,1,0:T(2,128)(2,1)} %get-tuple-element.10, f32[2,2,16,1024]{3,2,1,0:T(8,128)S(1)} %get-tuple-element.18, f32[2,2,16]{2,1,0:T(2,128)S(1)} %multiply_maximum_fusion, f32[2,2,16]{2,1,0:T(2,128)S(1)} %get-tuple-element.7, f32[2,2,128]{2,1,0:T(2,128)S(1)} %slice_bitcast_fusion, ...), kind=kOutput, calls=%fused_computation.10 | convolution fusion | flops 16941056 | bytes 1329920 | tf_op jit(solution)/shard_map/mrkgs,mrskd->mrkgd/dot_general | solution.py:53
  59.4 13.1 %all_gather.3 = bf16[2,8,2048]{2,0,1:T(2,128)(2,1)S(1)} all-gather(bf16[2,2,2048]{2,0,1:T(2,128)(2,1)S(1)} %copy.12), channel_id=1, replica_groups=mesh['groups'=2,'gx'=4,'gy'=4] {'gx'}, dimensions={1}, use_global_device_ids=true | all-gather | bytes 81920 | tf_op jit(solution)/shard_map/all_gather | solution.py:83
  72.6 8.8 %fusion = f32[2,8,4096]{2,1,0:T(8,128)} fusion(bf16[2048,4096]{1,0:T(8,128)(2,1)} %param.12, bf16[2,8,2048]{2,0,1:T(2,128)(2,1)S(1)} %all_gather.3), kind=kOutput, calls=%fused_computation | convolution fusion | flops 268435456 | bytes 17104896 | tf_op jit(solution)/shard_map/mrc,cd->mrd/dot_general | solution.py:81
  81.3 32.2 %all-reduce.7.cloned.1.call-done = f32[2,8,4096]{2,1,0:T(8,128)} async-done(((f32[2,8,4096]{2,1,0:T(8,128)}), f32[2,8,4096]{2,1,0:T(8,128)}) %all-reduce.7.cloned.1.call-update) | async-done | bytes 262160 | tf_op jit(solution)/shard_map/psum | solution.py:87
  113.5 1.6 %fusion.14 = bf16[2,8,4096]{2,1,0:T(8,128)(2,1)} fusion(f32[2,8,4096]{2,1,0:T(8,128)} %all-reduce.7.cloned.1.call-done, bf16[2,8,4096]{2,1,0:T(8,128)(2,1)S(1)} %copy-done.1), kind=kLoop, calls=%fused_computation.19 | loop fusion | flops 196608 | bytes 524288 | tf_op jit(solution)/shard_map/convert_element_type | solution.py:88
  (21 shorter events, 0.3 us)
Async XLA Ops:
  6.5 10.0 %copy-start = (bf16[4096,1,256]{2,0,1:T(8,128)(2,1)S(1)}, bf16[4096,1,256]{2,0,1:T(8,128)(2,1)}, u32[]{:S(2)}) copy-start(bf16[4096,1,256]{2,0,1:T(8,128)(2,1)} %param.11) | copy-start | bytes 6291460
  6.5 47.3 %all-reduce.9.cloned.1.call-start = ((), (), s32[]{:S(2)}) async-start(), calls=%async_computation.1 | async-start | bytes 262144
  7.4 8.9 %copy-start.1 = (bf16[2,8,4096]{2,1,0:T(8,128)(2,1)S(1)}, bf16[2,8,4096]{2,1,0:T(8,128)(2,1)}, u32[]{:S(2)}) copy-start(bf16[2,8,4096]{2,1,0:T(8,128)(2,1)} %param.7) | copy-start | bytes 393220
  7.4 9.0 %copy-start.2 = (s32[2,2]{1,0:T(2,128)S(1)}, s32[2,2]{1,0:T(2,128)}, u32[]{:S(2)}) copy-start(s32[2,2]{1,0:T(2,128)} %param.8) | copy-start | bytes 52
  16.2 0.7 copy-start.3
  16.2 97.3 %all-reduce.7.cloned.1.call-start = ((), (), s32[]{:S(2)}) async-start(), calls=%async_computation | async-start | bytes 524288 | tf_op jit(solution)/shard_map/psum | solution.py:87
Sparse Core Ops, SparseCore 0:
  16.4 37.4 all-reduce.8
  81.5 31.9 all-reduce.6
where the time goes:
time: 122 us
  waiting for transfers between devices  39.5 us (32%)
  blocking collectives  33.9 us (28%)
  matrix products  22 us (18%)
  between operations  14.2 us (12%)
  local copies, waits for them, and re-layouts  8.61 us (7%)
  other arithmetic  3.71 us (3%)
    psum x1, waiting for transfers between devices, local(): summed_heads = lax.psum(projected, 'gy')  32.2 us
    unnamed x1, blocking collectives  20.8 us
    all_gather x1, blocking collectives, local(): lax.all_gather(attended, 'gx', axis=1, tiled=True)  13.1 us
    dot_general x1, matrix products, local(): jnp.einsum('mrd,dc->mrc', normed, w_query, preferred_element_type=jnp.flo...  8.81 us
    dot_general x1, matrix products, local(): jnp.einsum('mrc,cd->mrd', lax.all_gather(attended, 'gx', axis=1, tiled=Tr...  8.75 us
    unnamed x3, waiting for transfers between devices  7.38 us
    slice x1, local copies, waits for them, and re-layouts, attend(): keys = cache[:, :, :, :, 0, :]  6.95 us
  transfers between devices with their start and end apart: 2, of which 2 were waited for; matrix products, arithmetic and copies ran while one was open for 7% of the time, Pallas kernels for 0%

commit v1 on v0

--- a/solution.py
+++ b/solution.py
@@ -2,9 +2,30 @@
 import jax.numpy as jnp
 from jax import lax
 from jax.sharding import PartitionSpec as P
+from jax.lax import axis_index, axis_size, ppermute
 
 MODEL_WIDTH = 16384
 HEAD_SIZE = 128
+
+
+def track_cells(t0, lane_axis, z):
+    clean = axis_size(lane_axis)
+    fresh, local_now, current_block = (clean, axis_index(lane_axis), t0.shape[1])
+    last, extra = ([], [])
+    now = v_now = t0
+    for tick in range(fresh // 2 + 1):
+        current_arr = z(now, (local_now - tick) % fresh * current_block)
+        last.append(current_arr)
+        if 0 < tick < fresh - fresh // 2:
+            extra.append(z(v_now, (local_now + tick) % fresh * current_block))
+        earlier = map(lambda ii: (ii, (ii + 1) % fresh), range(fresh))
+        now = ppermute(now, axis_name=lane_axis, perm=list(earlier))
+        local_out = range(fresh)
+        val2 = map(lambda ii: (ii, (ii - 1) % fresh), local_out)
+        v_now = ppermute(v_now, axis_name=lane_axis, perm=list(val2))
+    later = jnp.concatenate([*last[::-1], *extra], 1)
+    tile_out = jnp.roll(later, (local_now - fresh // 2) * last[0].shape[1], 1)
+    return tile_out
 
 
 def rotate(vectors, positions):
@@ -78,11 +99,12 @@
         lax.psum_scatter(squares, "gx", scatter_dimension=1, tiled=True),
     )
     attended = attend(query_sum, keyval_sum, local_squares, lengths, cache)
-    projected = jnp.einsum(
-        "mrc,cd->mrd",
-        lax.all_gather(attended, "gx", axis=1, tiled=True),
-        w_out,
-        preferred_element_type=jnp.float32,
+    projected = track_cells(
+        attended,
+        "gx",
+        lambda shard, start: jnp.einsum(
+            "mrc,cd->mrd", shard, w_out, preferred_element_type=jnp.float32
+        ),
     )
     summed_heads = lax.psum(projected, "gy")
     return (x_full + summed_heads).astype(jnp.bfloat16)

time: 122 us -> 128 us (1.049)
  matrix products: 22 us -> 35.2 us
  blocking collectives: 33.9 us -> 20.8 us
  starting transfers between devices: 0.04 us -> 3.79 us
    dot_general x1 -> x4, matrix products: 8.75 us -> 22 us  [local(): jnp.einsum('mrc,cd->mrd', shard, w_out, preferred_element_type=jnp.float32)]
    all_gather x1 -> x0, blocking collectives: 13.1 us -> none  [local(): lax.all_gather(attended, 'gx', axis=1, tiled=True)]
    ppermute x0 -> x3, starting transfers between devices: none -> 3.72 us  [the longest x1 2.18 us: track_cells(): v_now = ppermute(v_now, axis_name=lane_axis, perm=list(val2))]
  transfers between devices with their start and end apart: 2 -> 5, of which waited for: 2 -> 2; matrix products, arithmetic and copies ran while one was open for 7% -> 22% of each run, Pallas kernels for 0% -> 0%
where the time goes in v1:
time: 128 us
  waiting for transfers between devices  40.4 us (32%)
  matrix products  35.2 us (28%)
  blocking collectives  20.8 us (16%)
  between operations  14.2 us (11%)
  local copies, waits for them, and re-layouts  9.63 us (8%)
  starting transfers between devices  3.79 us (3%)
  other arithmetic  3.71 us (3%)
    psum x1, waiting for transfers between devices, local(): summed_heads = lax.psum(projected, 'gy')  32.7 us
    dot_general x4, matrix products, local(): jnp.einsum('mrc,cd->mrd', shard, w_out, preferred_element_type=jnp.float32)  22 us
    unnamed x1, blocking collectives  20.8 us
    dot_general x1, matrix products, local(): jnp.einsum('mrd,dc->mrc', normed, w_query, preferred_element_type=jnp.flo...  8.78 us
    unnamed x3, waiting for transfers between devices  7.69 us
    slice x1, local copies, waits for them, and re-layouts, attend(): keys = cache[:, :, :, :, 0, :]  6.89 us
  transfers between devices with their start and end apart: 5, of which 2 were waited for; matrix products, arithmetic and copies ran while one was open for 22% of the time, Pallas kernels for 0%

profile of v1, /device:TPU:0, one launch (start us, length us, event | category | flops | bytes accessed | tf_op | source)
XLA Modules:
  0.0 127.7 jit_solution(15194413661312202251)
XLA Ops:
  6.6 0.8 convert_element_type.46
  7.4 8.8 %fusion.8 = f32[2,8,2048]{2,1,0:T(8,128)} fusion(bf16[4096,2048]{1,0:T(8,128)(2,1)} %param.10, bf16[2,8,4096]{2,1,0:T(8,128)(2,1)} %param.7, f32[4096]{0:T(1024)S(1)} %convert_element_type.46), kind=kOutput, calls=%fused_computation.8 | convolution fusion | flops 268632064 | bytes 17055744 | tf_op jit(solution)/shard_map/mrd,dc->mrc/dot_general | solution.py:92
  16.3 0.1 fusion.19
  16.5 0.4 fusion.15
  16.9 0.6 dynamic-slice
  18.2 20.8 %all-reduce.3 = (f32[2,8]{1,0:T(2,128)S(1)}, f32[2,8,1,256]{3,1,0,2:T(8,128)S(1)}) all-reduce(f32[2,8]{1,0:T(2,128)S(1)} %fusion.19, f32[2,8,1,256]{3,1,0,2:T(8,128)S(1)} %fusion.15), channel_id=3, replica_groups=mesh['groups'=2,'gx'=4,'gy'=4] {'gx'}, use_global_device_ids=true, to_apply=%region_2.0.clone | all-reduce | flops 4112 | bytes 32896
  39.1 0.1 fusion.34
  39.3 6.9 %fusion.40 = (bf16[2,2,1024,1,1,128]{5,4,3,2,1,0:T(2,128)(2,1)}, bf16[2,2,1024,1,1,128]{5,4,3,2,1,0:T(2,128)(2,1)}) fusion(bf16[2,2,1024,1,2,128]{5,4,3,2,1,0:T(2,128)(2,1)} %param.13), kind=kLoop, calls=%fused_computation.61 | loop fusion | bytes 4194304 | tf_op jit(solution)/shard_map/slice | solution.py:59
  46.2 7.7 %all-reduce.9.cloned.1.call-done = f32[2,8,2048]{2,1,0:T(8,128)} async-done(((f32[2,8,2048]{2,1,0:T(8,128)}), f32[2,8,2048]{2,1,0:T(8,128)}) %all-reduce.9.cloned.1.call-update) | async-done | bytes 131088
  53.9 0.9 constant_dynamic-slice_fusion
  55.0 0.2 multiply_reduce_fusion
  55.2 2.1 %fusion.41 = (f32[2,2,16]{2,1,0:T(2,128)S(1)}, f32[2,2,16,1024]{3,2,1,0:T(8,128)S(1)}) fusion(bf16[2,2,1024,1,1,128]{5,4,3,2,1,0:T(2,128)(2,1)} %get-tuple-element.9, bf16[2,2,16,64]{3,2,1,0:T(8,128)(2,1)S(1)} %bitcast.50, bf16[2,2,16,64]{3,2,1,0:T(8,128)(2,1)S(1)} %bitcast.49, pred[2,2,1024]{2,1,0:T(4,128)(4,1)S(1)} %iota_compare_fusion), kind=kOutput, calls=%fused_computation.62 | convolution fusion | flops 17006528 | bytes 1331456 | tf_op jit(solution)/shard_map/mrkgd,mrskd->mrkgs/dot_general | solution.py:62
  57.3 0.2 fusion.21
  57.5 1.9 %fusion.14 = bf16[2,2,16,128]{3,2,1,0:T(8,128)(2,1)S(1)} fusion(bf16[2,2,1024,1,1,128]{5,4,3,2,1,0:T(2,128)(2,1)} %get-tuple-element.10, f32[2,2,16,1024]{3,2,1,0:T(8,128)S(1)} %get-tuple-element.18, f32[2,2,16]{2,1,0:T(2,128)S(1)} %multiply_maximum_fusion, f32[2,2,16]{2,1,0:T(2,128)S(1)} %get-tuple-element.7, f32[2,2,128]{2,1,0:T(2,128)S(1)} %slice_bitcast_fusion, ...), kind=kOutput, calls=%fused_computation.16 | convolution fusion | flops 16941056 | bytes 1329920 | tf_op jit(solution)/shard_map/mrkgs,mrskd->mrkgd/dot_general | solution.py:74
  59.5 2.2 %collective-permute-start.2 = (bf16[2,2,2048]{2,1,0:T(2,128)(2,1)S(1)}, bf16[2,2,2048]{2,1,0:T(2,128)(2,1)S(1)}, u32[]{:S(2)}, u32[]{:S(2)}) collective-permute-start(bf16[2,2,2048]{2,1,0:T(2,128)(2,1)S(1)} %reshape.199), channel_id=1, source_target_pairs={{0,12},{4,0},{8,4},{12,8},{1,13},{5,1},{9,5},{13,9},{2,14},{6,2},{... | collective-permute-start | bytes 49160 | tf_op jit(solution)/shard_map/ppermute | solution.py:25
  61.7 8.9 %fusion.2 = f32[2,2,4096]{2,1,0:T(2,128)S(1)} fusion(bf16[2,2,2048]{2,1,0:T(2,128)(2,1)S(1)} %reshape.199, bf16[2048,4096]{1,0:T(8,128)(2,1)} %param.12), kind=kOutput, calls=%fused_computation.2 | convolution fusion | flops 67108864 | bytes 16859136 | tf_op jit(solution)/shard_map/mrc,cd->mrd/dot_general | solution.py:105
  70.6 1.5 %collective-permute-start.1 = (bf16[2,2,2048]{2,1,0:T(2,128)(2,1)S(1)}, bf16[2,2,2048]{2,1,0:T(2,128)(2,1)S(1)}, u32[]{:S(2)}, u32[]{:S(2)}) collective-permute-start(bf16[2,2,2048]{2,1,0:T(2,128)(2,1)S(1)} %collective-permute-done), channel_id=1, source_target_pairs={{0,4},{4,8},{8,12},{12,0},{1,5},{5,9},{9,13},{13,1},{2,6},{6,10},{... | collective-permute-start | bytes 49160 | tf_op jit(solution)/shard_map/ppermute | solution.py:22
  72.2 8.2 %fusion.4 = f32[2,2,4096]{2,1,0:T(2,128)S(1)} fusion(bf16[2,2,2048]{2,1,0:T(2,128)(2,1)S(1)} %collective-permute-done, bf16[2048,4096]{1,0:T(8,128)(2,1)} %param.12), kind=kOutput, calls=%fused_computation.4 | convolution fusion | flops 67108864 | bytes 16859136 | tf_op jit(solution)/shard_map/mrc,cd->mrd/dot_general | solution.py:105
  80.4 2.5 %fusion = f32[2,2,4096]{2,1,0:T(2,128)S(1)} fusion(bf16[2,2,2048]{2,1,0:T(2,128)(2,1)S(1)} %collective-permute-done.2, bf16[2048,4096]{1,0:T(8,128)(2,1)S(1)} %bitcast.48), kind=kOutput, calls=%fused_computation | convolution fusion | flops 67108864 | bytes 16859136 | tf_op jit(solution)/shard_map/mrc,cd->mrd/dot_general | solution.py:105
  82.8 2.5 %fusion.6 = f32[2,2,4096]{2,1,0:T(2,128)S(1)} fusion(bf16[2,2,2048]{2,1,0:T(2,128)(2,1)S(1)} %collective-permute-done.1, bf16[2048,4096]{1,0:T(8,128)(2,1)S(1)} %bitcast.48), kind=kOutput, calls=%fused_computation.6 | convolution fusion | flops 67108864 | bytes 16859136 | tf_op jit(solution)/shard_map/mrc,cd->mrd/dot_general | solution.py:105
  85.3 0.4 concatenate.35
  85.7 0.7 constant_dynamic-slice_fusion.1
  86.5 32.7 %all-reduce.7.cloned.1.call-done = f32[2,8,4096]{2,1,0:T(8,128)} async-done(((f32[2,8,4096]{2,1,0:T(8,128)}), f32[2,8,4096]{2,1,0:T(8,128)}) %all-reduce.7.cloned.1.call-update) | async-done | bytes 262160 | tf_op jit(solution)/shard_map/psum | solution.py:109
  119.2 1.6 %fusion.20 = bf16[2,8,4096]{2,1,0:T(8,128)(2,1)} fusion(f32[2,8,4096]{2,1,0:T(8,128)} %all-reduce.7.cloned.1.call-done, bf16[2,8,4096]{2,1,0:T(8,128)(2,1)S(1)} %copy-done.1), kind=kLoop, calls=%fused_computation.25 | loop fusion | flops 196608 | bytes 524288 | tf_op jit(solution)/shard_map/convert_element_type | solution.py:110
  (39 shorter events, 0.8 us)
Async XLA Ops:
  6.5 10.0 %copy-start = (bf16[4096,1,256]{2,0,1:T(8,128)(2,1)S(1)}, bf16[4096,1,256]{2,0,1:T(8,128)(2,1)}, u32[]{:S(2)}) copy-start(bf16[4096,1,256]{2,0,1:T(8,128)(2,1)} %param.11) | copy-start | bytes 6291460
  6.5 10.4 %copy-start.3 = (u32[32]{0:T(128)S(1)}, u32[32]{0:T(128)}, u32[]{:S(2)}) copy-start(u32[32]{0:T(128)} %constant.58) | copy-start | bytes 388
  6.5 9.8 %copy-start.1 = (bf16[2,8,4096]{2,1,0:T(8,128)(2,1)S(1)}, bf16[2,8,4096]{2,1,0:T(8,128)(2,1)}, u32[]{:S(2)}) copy-start(bf16[2,8,4096]{2,1,0:T(8,128)(2,1)} %param.7) | copy-start | bytes 393220
  6.5 9.9 %copy-start.2 = (s32[2,2]{1,0:T(2,128)S(1)}, s32[2,2]{1,0:T(2,128)}, u32[]{:S(2)}) copy-start(s32[2,2]{1,0:T(2,128)} %param.8) | copy-start | bytes 52
  6.5 47.3 %all-reduce.9.cloned.1.call-start = ((), (), s32[]{:S(2)}) async-start(), calls=%async_computation.1 | async-start | bytes 262144
  16.2 103.0 %all-reduce.7.cloned.1.call-start = ((), (), s32[]{:S(2)}) async-start(), calls=%async_computation | async-start | bytes 524288 | tf_op jit(solution)/shard_map/psum | solution.py:109
  59.4 20.9 %slice-start = ((s8[16777216]{0:T(1024)(128)(4,1)}), s8[4194304]{0:T(1024)(128)(4,1)S(1)}, s32[]{:S(2)}) async-start(s8[16777216]{0:T(1024)(128)(4,1)} %bitcast.47), calls=%async_computation.2 | async-start | bytes 8388608
  59.5 20.9 %slice-start.1 = ((s8[16777216]{0:T(1024)(128)(4,1)}), s8[4194304]{0:T(1024)(128)(4,1)S(1)}, s32[]{:S(2)}) async-start(s8[16777216]{0:T(1024)(128)(4,1)} %bitcast.47), calls=%async_computation.3 | async-start | bytes 8388608
  59.5 20.9 %slice-start.2 = ((s8[16777216]{0:T(1024)(128)(4,1)}), s8[4194304]{0:T(1024)(128)(4,1)S(1)}, s32[]{:S(2)}) async-start(s8[16777216]{0:T(1024)(128)(4,1)} %bitcast.47), calls=%async_computation.4 | async-start | bytes 8388608
  59.5 20.8 %collective-permute-start.2 = (bf16[2,2,2048]{2,1,0:T(2,128)(2,1)S(1)}, bf16[2,2,2048]{2,1,0:T(2,128)(2,1)S(1)}, u32[]{:S(2)}, u32[]{:S(2)}) collective-permute-start(bf16[2,2,2048]{2,1,0:T(2,128)(2,1)S(1)} %reshape.199), channel_id=1, source_target_pairs={{0,12},{4,0},{8,4},{12,8},{1,13},{5,1},{9,5},{13,9},{2,14},{6,2},{... | collective-permute-start | bytes 49160 | tf_op jit(solution)/shard_map/ppermute | solution.py:25
  61.7 9.0 %collective-permute-start = (bf16[2,2,2048]{2,1,0:T(2,128)(2,1)S(1)}, bf16[2,2,2048]{2,1,0:T(2,128)(2,1)S(1)}, u32[]{:S(2)}, u32[]{:S(2)}) collective-permute-start(bf16[2,2,2048]{2,1,0:T(2,128)(2,1)S(1)} %reshape.199), channel_id=1, source_target_pairs={{0,4},{4,8},{8,12},{12,0},{1,5},{5,9},{9,13},{13,1},{2,6},{6,10},{... | collective-permute-start | bytes 49160 | tf_op jit(solution)/shard_map/ppermute | solution.py:22
  70.6 9.8 %slice-start.3 = ((s8[16777216]{0:T(1024)(128)(4,1)}), s8[4194304]{0:T(1024)(128)(4,1)S(1)}, s32[]{:S(2)}) async-start(s8[16777216]{0:T(1024)(128)(4,1)} %bitcast.47), calls=%async_computation.5 | async-start | bytes 8388608
  70.6 12.2 %collective-permute-start.1 = (bf16[2,2,2048]{2,1,0:T(2,128)(2,1)S(1)}, bf16[2,2,2048]{2,1,0:T(2,128)(2,1)S(1)}, u32[]{:S(2)}, u32[]{:S(2)}) collective-permute-start(bf16[2,2,2048]{2,1,0:T(2,128)(2,1)S(1)} %collective-permute-done), channel_id=1, source_target_pairs={{0,4},{4,8},{8,12},{12,0},{1,5},{5,9},{9,13},{13,1},{2,6},{6,10},{... | collective-permute-start | bytes 49160 | tf_op jit(solution)/shard_map/ppermute | solution.py:22
Sparse Core Ops, SparseCore 0:
  16.4 37.4 all-reduce.8
  86.6 32.5 all-reduce.6
